TPU v7x, 32 devices: a whole 2x2x4 slice. The times are simulated.
32 devices in a mesh: pts: 8 (over z, core), head: 4 (over y, x).
Axes of the slice: x: 2, y: 2, z: 4, core: 2. Of those that a mesh axis runs over, the one named last changes fastest.
Arguments:
- points: bfloat16 [73728, 128], P('pts')
- counts: int32 [8], P('pts'), may hold values from 1 to 9216, 55296 in all
- ln1_gain: float32 [2, 128], replicated, may hold values from 0.5 to 1.5
- ln1_bias: float32 [2, 128], replicated, may hold values from -1.5 to 1.5
- w_in: bfloat16 [2, 128, 128], P(None, None, 'head'), may hold values from -0.5 to 0.5
- w_fx: bfloat16 [2, 128, 128], P(None, None, 'head'), may hold values from -0.5 to 0.5
- w_slice: bfloat16 [2, 32, 32], replicated
- temper: float32 [2, 4], replicated, may hold values from 0.5 to 2
- query_weight: bfloat16 [2, 32, 32], replicated
- key_weight: bfloat16 [2, 32, 32], replicated, may hold values from -1 to 1
- value_weight: bfloat16 [2, 32, 32], replicated, may hold values from -1 to 1
- w_out: bfloat16 [2, 128, 128], P(None, 'head'), may hold values from -1 to 1
- b_out: float32 [2, 128], replicated, may hold values from -1.5 to 1.5
- ln2_gain: float32 [2, 128], replicated, may hold values from 0.5 to 1.5
- ln2_bias: float32 [2, 128], replicated, may hold values from -1.5 to 1.5
- w_up: bfloat16 [2, 128, 512], replicated, may hold values from -0.5 to 0.5
- w_down: bfloat16 [2, 512, 128], replicated, may hold values from -0.25 to 0.25
Outputs:
- features: bfloat16 [73728, 128], P(('pts', 'head'))
Inputs may be any that keep to these rules, and one draw needn't show every extreme that they name: counts[i] live points fill the first slots of shard i; at least one shard is full; they sum to 55296.
All inputs are finite; a program needn't handle non-finite values.
Results may differ from a plain program's by a relative error of at most 0.014.
Values may be sent and summed in bfloat16 or wider, within the bound.
A program may use at most 128 MiB of HBM per device.

v0:
```python
import jax
import jax.numpy as jnp
from jax import lax
from jax.sharding import PartitionSpec as P

DH = 32
M = 32


def layer_norm(value, gain, bias):
    mean = jnp.mean(value, axis=-1, keepdims=True)
    centred = value - mean
    var = jnp.mean(centred * centred, axis=-1, keepdims=True)
    return centred * lax.rsqrt(var + 1e-05) * gain + bias


def slice_attention(token_rows, query_weight, key_weight, value_weight):
    head_parts = lax.Precision.HIGHEST
    query_rows = jnp.einsum(
        "aur,rz->auz", token_rows, query_weight.astype(jnp.float32), precision=head_parts
    )
    slice_keys = jnp.einsum(
        "aur,rz->auz", token_rows, key_weight.astype(jnp.float32), precision=head_parts
    )
    slice_values = jnp.einsum(
        "aur,rz->auz", token_rows, value_weight.astype(jnp.float32), precision=head_parts
    )
    scores = jnp.einsum("hme,hke->hmk", query_rows, slice_keys, precision=head_parts) * DH ** (-0.5)
    attn = jax.nn.softmax(scores, axis=-1)
    return jnp.einsum("hmk,hke->hme", attn, slice_values, precision=head_parts).astype(jnp.bfloat16)


def body(
    points,
    counts,
    ln1_gain,
    ln1_bias,
    w_in,
    w_fx,
    w_slice,
    temper,
    query_weight,
    key_weight,
    value_weight,
    w_out,
    b_out,
    ln2_gain,
    ln2_bias,
    w_up,
    w_down,
):
    groups = lax.axis_size("head")
    rows = points.shape[0] // groups
    first_row = lax.axis_index("head") * rows
    layers = w_in.shape[0]
    full_in = lax.all_gather(w_in, "head", axis=2, tiled=True)
    full_fx = lax.all_gather(w_fx, "head", axis=2, tiled=True)
    full_out = lax.all_gather(w_out, "head", axis=1, tiled=True)
    heads = full_in.shape[2] // DH
    live = (first_row + jnp.arange(rows, dtype=jnp.int32) < counts[0]).astype(jnp.float32)
    current = lax.dynamic_slice_in_dim(points, first_row, rows, 0)
    for layer_index in range(layers):
        normed = layer_norm(
            current.astype(jnp.float32), ln1_gain[layer_index], ln1_bias[layer_index]
        ).astype(jnp.bfloat16)
        mid = jnp.dot(normed, full_in[layer_index], preferred_element_type=jnp.float32).astype(
            jnp.bfloat16
        )
        feats = jnp.dot(normed, full_fx[layer_index], preferred_element_type=jnp.float32).astype(
            jnp.bfloat16
        )
        spread = jnp.kron(jnp.eye(heads, dtype=jnp.bfloat16), w_slice[layer_index])
        logits = jnp.dot(mid, spread, preferred_element_type=jnp.float32)
        logits = logits.reshape(rows, heads, M) / temper[layer_index][None, :, None]
        weights = jax.nn.softmax(logits, axis=-1) * live[:, None, None]
        half_weights = weights.astype(jnp.bfloat16).reshape(rows, heads * M)
        total = jnp.sum(weights, axis=0)
        square = jnp.einsum("rs,rl->sl", half_weights, feats, preferred_element_type=jnp.float32)
        square = square.reshape(heads, M, heads, DH)
        numerator = jnp.stack([square[h, :, h, :] for h in range(heads)])
        numerator, total = lax.psum((numerator, total), ("pts", "head"))
        token_rows = numerator / jnp.maximum(total, 1.0)[..., None]
        mixed_token = slice_attention(
            token_rows,
            query_weight[layer_index],
            key_weight[layer_index],
            value_weight[layer_index],
        )
        wide = (
            jnp.einsum(
                "hmv,hvc->hmc",
                mixed_token,
                full_out[layer_index].reshape(heads, DH, -1),
                preferred_element_type=jnp.float32,
            )
            .astype(jnp.bfloat16)
            .reshape(heads * M, -1)
        )
        projected = jnp.dot(half_weights, wide, preferred_element_type=jnp.float32)
        after = current.astype(jnp.float32) + projected + b_out[layer_index]
        normed2 = layer_norm(after, ln2_gain[layer_index], ln2_bias[layer_index]).astype(
            jnp.bfloat16
        )
        upper = jax.nn.gelu(
            jnp.dot(normed2, w_up[layer_index], preferred_element_type=jnp.float32)
        ).astype(jnp.bfloat16)
        current = (
            after + jnp.dot(upper, w_down[layer_index], preferred_element_type=jnp.float32)
        ).astype(jnp.bfloat16)
    return current


def solution(mesh):
    placed = (
        P("pts", None),
        P("pts"),
        P(),
        P(),
        P(None, None, "head"),
        P(None, None, "head"),
        P(),
        P(),
        P(),
        P(),
        P(),
        P(None, "head", None),
        P(),
        P(),
        P(),
        P(),
        P(),
    )
    return jax.shard_map(
        body, mesh=mesh, in_specs=placed, out_specs=P(("pts", "head"), None), check_vma=False
    )
```

profile of v0, /device:TPU:0, one launch (start us, length us, event | category | flops | bytes accessed | tf_op | source)
XLA Modules:
  0.0 157.5 jit_solution(5383199505180625222)
XLA Ops:
  0.0 1.7 %copy-done = bf16[9216,128]{1,0:T(8,128)(2,1)S(1)} copy-done((bf16[9216,128]{1,0:T(8,128)(2,1)S(1)}, bf16[9216,128]{1,0:T(8,128)(2,1)}, u32[]{:S(2)}) %copy-start) | copy-done | bytes 2359320
  3.5 0.8 broadcast_multiply_fusion
  4.4 9.7 %all_gather.9 = bf16[2,128,128]{1,2,0:T(8,128)(2,1)S(1)} all-gather(bf16[2,128,32]{1,2,0:T(8,128)(2,1)S(1)} %copy-done.10), channel_id=1, replica_groups=mesh['pts'=8,'head'=4] {'head'}, dimensions={2}, use_global_device_ids=true | all-gather | bytes 81920 | tf_op jit(solution)/shard_map/all_gather | solution.py:56
  14.2 1.9 %fusion.122 = (f32[2304,4]{0,1:T(4,128)S(1)}, f32[2304,4,32]{0,2,1:T(8,128)}) fusion(bf16[4,32,128]{2,1,0:T(8,128)(2,1)S(1)} %bitcast.209, f32[4]{0:T(128)S(1)} %get-tuple-element.28, bf16[2,128,128]{1,2,0:T(8,128)(2,1)S(1)} %all_gather.9, bf16[2304,128]{0,1:T(8,128)(2,1)S(1)} %copy.26, f32[128]{0:T(128)S(1)} %get-tuple-element.34, ...), kind=kOutput, calls=%fused_computation.175 | convolution fusion | flops 153944096 | bytes 1897984 | tf_op jit(solution)/shard_map/sub | solution.py:75
  16.7 1.6 %fusion.57 = f32[4,32]{1,0:T(4,128)S(1)} fusion(f32[2304]{0:T(1024)S(1)} %fusion.83, f32[2304,4,32]{0,2,1:T(8,128)} %get-tuple-element.36, f32[2304,4]{0,1:T(4,128)S(1)} %get-tuple-element.35), kind=kLoop, calls=%fused_computation.77 | loop fusion | flops 884608 | bytes 1226240 | tf_op jit(solution)/shard_map/reduce_sum | solution.py:77
  18.3 8.2 %all_gather.10 = bf16[2,128,128]{1,2,0:T(8,128)(2,1)S(1)} all-gather(bf16[2,128,32]{1,2,0:T(8,128)(2,1)S(1)} %copy-done.11), channel_id=1, replica_groups=mesh['pts'=8,'head'=4] {'head'}, dimensions={2}, use_global_device_ids=true | all-gather | bytes 81920 | tf_op jit(solution)/shard_map/all_gather | solution.py:57
  27.0 0.6 fusion.39
  27.7 40.2 %all-reduce.1 = (f32[4,32,32]{2,1,0:T(8,128)S(1)}, f32[4,32]{1,0:T(4,128)S(1)}) all-reduce(f32[4,32,32]{2,1,0:T(8,128)S(1)} %pad_maximum_fusion, f32[4,32]{1,0:T(4,128)S(1)} %fusion.57), channel_id=1, replica_groups=mesh['pts'=8,'head'=4] {'pts','head'}, use_global_device_ids=true, to_apply=%region_4.5 | all-reduce | flops 4224 | bytes 33792 | tf_op jit(solution)/shard_map/psum | solution.py:81
  69.3 9.0 %all_gather.11 = bf16[2,128,128]{2,1,0:T(8,128)(2,1)S(1)} all-gather(bf16[2,32,128]{2,1,0:T(8,128)(2,1)S(1)} %copy-done.12), channel_id=1, replica_groups=mesh['pts'=8,'head'=4] {'head'}, dimensions={1}, use_global_device_ids=true | all-gather | bytes 81920 | tf_op jit(solution)/shard_map/all_gather | solution.py:58
  78.3 0.6 fusion.121
  79.4 2.8 %fusion.126 = (f32[2304]{0:T(1024)S(1)}, f32[2304,128]{0,1:T(8,128)}) fusion(f32[128]{0:T(128)S(1)} %get-tuple-element.26, bf16[4,32,32]{2,1,0:T(8,128)(2,1)S(1)} %convolution_convert_fusion.7, bf16[4,32,128]{2,1,0:T(8,128)(2,1)S(1)} %bitcast.212, f32[2304]{0:T(1024)S(1)} %fusion.83, f32[2304,4,32]{0,2,1:T(8,128)} %get-tuple-element.36, ...), kind=kOutput, calls=%fused_computation.177 | convolution fusion | flops 78624512 | bytes 3045888 | tf_op jit(solution)/shard_map/dot_general | solution.py:99
  82.2 1.4 multiply_reduce_fusion.2
  83.6 0.6 add_rsqrt_fusion.2
  84.8 4.6 %fusion.127 = (f32[2304]{0:T(1024)}, f32[2304,128]{0,1:T(8,128)S(1)}) fusion(f32[2304,128]{0,1:T(8,128)} %get-tuple-element.40, bf16[2,512,128]{2,1,0:T(8,128)(2,1)} %param.33, f32[128]{0:T(128)} %get-tuple-element.24, f32[128]{0:T(128)} %get-tuple-element.51, f32[2304]{0:T(1024)} %add_rsqrt_fusion.2, f32[2304]{0:T(1024)} %copy-done.8, ...), kind=kOutput, calls=%fused_computation.178 | convolution fusion | flops 617248512 | bytes 3835904 | tf_op jit(solution)/shard_map/dot_general | solution.py:108
  89.4 0.7 broadcast_multiply_fusion.3
  90.3 1.2 add_convert_fusion.1
  91.5 1.6 %mul.210 = bf16[128,128]{0,1:T(8,128)(2,1)} reshape(bf16[4,32,4,32]{1,0,3,2:T(4,128)(2,1)} %get-tuple-element.29) | data formatting | bytes 65536 | tf_op jit(solution)/shard_map/jit(kron)/mul | solution.py:72
  93.1 3.4 %fusion.130 = (f32[2304,4]{0,1:T(4,128)}, f32[2304,4,32]{0,2,1:T(8,128)}) fusion(bf16[4,32,128]{2,1,0:T(8,128)(2,1)} %bitcast.210, bf16[2304,128]{0,1:T(8,128)(2,1)} %add_convert_fusion.1, f32[4]{0:T(128)S(1)} %get-tuple-element.27, bf16[2,128,128]{1,2,0:T(8,128)(2,1)} %copy-done.7), kind=kOutput, calls=%fused_computation.179 | convolution fusion | flops 152174624 | bytes 1871888 | tf_op jit(solution)/shard_map/sub | solution.py:75
  96.5 1.6 %fusion.59 = f32[4,32]{1,0:T(4,128)S(1)} fusion(f32[2304]{0:T(1024)S(1)} %fusion.83, f32[2304,4,32]{0,2,1:T(8,128)} %get-tuple-element.44, f32[2304,4]{0,1:T(4,128)} %get-tuple-element.43), kind=kLoop, calls=%fused_computation.79 | loop fusion | flops 884608 | bytes 1226240 | tf_op jit(solution)/shard_map/reduce_sum | solution.py:77
  99.1 0.6 pad_maximum_fusion.1
  99.7 40.3 %all-reduce = (f32[4,32,32]{2,1,0:T(8,128)}, f32[4,32]{1,0:T(4,128)}) all-reduce(f32[4,32,32]{2,1,0:T(8,128)} %pad_maximum_fusion.1, f32[4,32]{1,0:T(4,128)S(1)} %fusion.59), channel_id=1, replica_groups=mesh['pts'=8,'head'=4] {'pts','head'}, use_global_device_ids=true, to_apply=%region_15.16 | all-reduce | flops 4224 | bytes 33792 | tf_op jit(solution)/shard_map/psum | solution.py:81
  140.0 0.7 broadcast_maximum_fusion
  140.7 1.1 fusion.86
  141.8 1.1 fusion.88
  143.1 1.1 fusion.84
  144.2 0.9 convolution_convert_fusion.5
  145.2 3.4 %fusion.132 = (f32[2304]{0:T(1024)}, f32[2304,128]{0,1:T(8,128)}) fusion(f32[128]{0:T(128)} %get-tuple-element.25, f32[2304,128]{0,1:T(8,128)S(1)} %get-tuple-element.42, bf16[4,32,32]{2,1,0:T(8,128)(2,1)} %convolution_convert_fusion.5, bf16[4,32,128]{2,1,0:T(8,128)(2,1)} %bitcast.211, f32[2304]{0:T(1024)S(1)} %fusion.83, ...), kind=kOutput, calls=%fused_computation.181 | convolution fusion | flops 78329600 | bytes 3635712 | tf_op jit(solution)/shard_map/dot_general | solution.py:99
  148.6 0.8 broadcast_multiply_fusion.2
  149.4 1.4 multiply_reduce_fusion
  150.8 0.6 add_rsqrt_fusion
  151.4 4.0 %fusion.27 = bf16[2304,128]{0,1:T(8,128)(2,1)} fusion(f32[2304,128]{0,1:T(8,128)S(1)} %copy-done.4, f32[128]{0:T(128)S(1)} %copy-done.22, f32[128]{0:T(128)} %get-tuple-element.52, f32[2304]{0:T(1024)} %add_rsqrt_fusion, f32[2304]{0:T(1024)S(1)} %broadcast_multiply_fusion.2, bf16[2,512,128]{2,1,0:T(8,128)(2,1)} %param.33, bf16[2,128,512]{2,1,0:T(8,128)(2,1)} %param.32), kind=kOutput, calls=%fused_computation.35 | convolution fusion | flops 616660992 | bytes 3236864 | tf_op jit(solution)/shard_map/dot_general | solution.py:108
  155.4 2.1 %copy.22 = bf16[2304,128]{1,0:T(8,128)(2,1)} copy(bf16[2304,128]{0,1:T(8,128)(2,1)} %fusion.27) | data formatting | bytes 1179648 | tf_op jit(solution)/shard_map/convert_element_type | solution.py:109
  (85 shorter events, 6.1 us)
Async XLA Ops:
  0.0 1.7 %copy-start = (bf16[9216,128]{1,0:T(8,128)(2,1)S(1)}, bf16[9216,128]{1,0:T(8,128)(2,1)}, u32[]{:S(2)}) copy-start(bf16[9216,128]{1,0:T(8,128)(2,1)} %param.17) | copy-start | bytes 7077892
  1.7 1.6 copy-start.13
  2.0 0.7 copy-start.18
  2.0 0.7 copy-start.19
  2.0 2.4 %copy-start.10 = (bf16[2,128,32]{1,2,0:T(8,128)(2,1)S(1)}, bf16[2,128,32]{1,2,0:T(8,128)(2,1)}, u32[]{:S(2)}) copy-start(bf16[2,128,32]{1,2,0:T(8,128)(2,1)} %param.21) | copy-start | bytes 49156
  2.0 12.1 %copy-start.16 = (f32[2,4]{1,0:T(2,128)S(1)}, f32[2,4]{1,0:T(2,128)}, u32[]{:S(2)}) copy-start(f32[2,4]{1,0:T(2,128)} %param.24) | copy-start | bytes 100
  14.1 1.9 %copy-start.7 = (bf16[2,128,128]{1,2,0:T(8,128)(2,1)}, bf16[2,128,128]{1,2,0:T(8,128)(2,1)S(1)}, u32[]{:S(2)}) copy-start(bf16[2,128,128]{1,2,0:T(8,128)(2,1)S(1)} %all_gather.9) | copy-start | bytes 196612
  16.0 2.3 %copy-start.11 = (bf16[2,128,32]{1,2,0:T(8,128)(2,1)S(1)}, bf16[2,128,32]{1,2,0:T(8,128)(2,1)}, u32[]{:S(2)}) copy-start(bf16[2,128,32]{1,2,0:T(8,128)(2,1)} %param.22) | copy-start | bytes 49156
  16.7 10.3 %copy-start.2 = (f32[2304,4,32]{0,2,1:T(8,128)S(1)}, f32[2304,4,32]{0,2,1:T(8,128)}, u32[]{:S(2)}) copy-start(f32[2304,4,32]{0,2,1:T(8,128)} %get-tuple-element.36) | copy-start | bytes 3538948
  26.5 1.1 copy-start.5
  27.0 40.9 %copy-start.23 = (bf16[2,32,32]{2,1,0:T(8,128)(2,1)S(1)}, bf16[2,32,32]{2,1,0:T(8,128)(2,1)}, u32[]{:S(2)}) copy-start(bf16[2,32,32]{2,1,0:T(8,128)(2,1)} %param.26) | copy-start | bytes 12292
  27.0 41.2 %copy-start.24 = (bf16[2,32,32]{2,1,0:T(8,128)(2,1)S(1)}, bf16[2,32,32]{2,1,0:T(8,128)(2,1)}, u32[]{:S(2)}) copy-start(bf16[2,32,32]{2,1,0:T(8,128)(2,1)} %param.25) | copy-start | bytes 12292
  27.0 41.7 %copy-start.25 = (bf16[2,32,32]{2,1,0:T(8,128)(2,1)S(1)}, bf16[2,32,32]{2,1,0:T(8,128)(2,1)}, u32[]{:S(2)}) copy-start(bf16[2,32,32]{2,1,0:T(8,128)(2,1)} %param.27) | copy-start | bytes 12292
  27.6 41.6 %copy-start.12 = (bf16[2,32,128]{2,1,0:T(8,128)(2,1)S(1)}, bf16[2,32,128]{2,1,0:T(8,128)(2,1)}, u32[]{:S(2)}) copy-start(bf16[2,32,128]{2,1,0:T(8,128)(2,1)} %param.28) | copy-start | bytes 49156
  27.6 51.2 %copy-start.17 = (f32[2,128]{1,0:T(2,128)S(1)}, f32[2,128]{1,0:T(2,128)}, u32[]{:S(2)}) copy-start(f32[2,128]{1,0:T(2,128)} %param.29) | copy-start | bytes 3076
  82.2 2.1 %copy-start.20 = (f32[2,128]{1,0:T(2,128)S(1)}, f32[2,128]{1,0:T(2,128)}, u32[]{:S(2)}) copy-start(f32[2,128]{1,0:T(2,128)} %param.31) | copy-start | bytes 3076
  82.2 2.1 %copy-start.21 = (f32[2,128]{1,0:T(2,128)S(1)}, f32[2,128]{1,0:T(2,128)}, u32[]{:S(2)}) copy-start(f32[2,128]{1,0:T(2,128)} %param.30) | copy-start | bytes 3076
  82.2 2.7 %copy-start.8 = (f32[2304]{0:T(1024)}, f32[2304]{0:T(1024)S(1)}, u32[]{:S(2)}) copy-start(f32[2304]{0:T(1024)S(1)} %broadcast_multiply_fusion.4) | copy-start | bytes 27652
  89.4 0.9 copy-start.14
  89.4 0.9 copy-start.15
  96.5 1.6 %copy-start.1 = (bf16[2304,128]{0,1:T(8,128)(2,1)S(1)}, bf16[2304,128]{0,1:T(8,128)(2,1)}, u32[]{:S(2)}) copy-start(bf16[2304,128]{0,1:T(8,128)(2,1)} %add_convert_fusion.1) | copy-start | bytes 1769476
  96.5 1.6 %copy-start.6 = (bf16[2,128,128]{1,2,0:T(8,128)(2,1)S(1)}, bf16[2,128,128]{1,2,0:T(8,128)(2,1)}, u32[]{:S(2)}) copy-start(bf16[2,128,128]{1,2,0:T(8,128)(2,1)} %copy-done.5) | copy-start | bytes 196612
  96.5 2.0 %copy-start.3 = (f32[2304,4,32]{0,2,1:T(8,128)S(1)}, f32[2304,4,32]{0,2,1:T(8,128)}, u32[]{:S(2)}) copy-start(f32[2304,4,32]{0,2,1:T(8,128)} %get-tuple-element.44) | copy-start | bytes 3538948
  96.5 2.0 %copy-start.9 = (f32[2304,4]{0,1:T(4,128)S(1)}, f32[2304,4]{0,1:T(4,128)}, u32[]{:S(2)}) copy-start(f32[2304,4]{0,1:T(4,128)} %get-tuple-element.43) | copy-start | bytes 110596
  148.6 2.8 %copy-start.4 = (f32[2304,128]{0,1:T(8,128)S(1)}, f32[2304,128]{0,1:T(8,128)}, u32[]{:S(2)}) copy-start(f32[2304,128]{0,1:T(8,128)} %get-tuple-element.48) | copy-start | bytes 3538948
  148.6 2.8 %copy-start.22 = (f32[128]{0:T(128)S(1)}, f32[128]{0:T(128)}, u32[]{:S(2)}) copy-start(f32[128]{0:T(128)} %get-tuple-element.23) | copy-start | bytes 1540
where the time goes:
time: 159 us; the launch traced here: 158 us
  blocking collectives  107 us (67%)
  matrix products  27.6 us (17%)
  other arithmetic  12.6 us (8%)
  local copies, waits for them, and re-layouts  8.79 us (6%)
    psum x2, blocking collectives, body(): numerator, total = lax.psum((numerator, total), ('pts', 'head'))  80.5 us
    all_gather x1, blocking collectives, body(): full_in = lax.all_gather(w_in, 'head', axis=2, tiled=True)  9.72 us
    all_gather x1, blocking collectives, body(): full_out = lax.all_gather(w_out, 'head', axis=1, tiled=True)  9 us
    dot_general x2, matrix products, body(): jnp.dot(upper, w_down[layer_index], preferred_element_type=jnp.float32)  8.51 us
    all_gather x1, blocking collectives, body(): full_fx = lax.all_gather(w_fx, 'head', axis=2, tiled=True)  8.21 us
    dot_general x2, matrix products, body(): projected = jnp.dot(half_weights, wide, preferred_element_type=jnp.float32)  6.22 us
    sub x2, matrix products, body(): weights = jax.nn.softmax(logits, axis=-1) * live[:, None, None]  5.29 us
    reduce_sum x2, other arithmetic, body(): total = jnp.sum(weights, axis=0)  3.22 us

commit v1 on v0

--- a/solution.py
+++ b/solution.py
@@ -2,6 +2,7 @@
 import jax.numpy as jnp
 from jax import lax
 from jax.sharding import PartitionSpec as P
+from jax.lax import all_gather
 
 DH = 32
 M = 32
@@ -53,7 +54,7 @@
     rows = points.shape[0] // groups
     first_row = lax.axis_index("head") * rows
     layers = w_in.shape[0]
-    full_in = lax.all_gather(w_in, "head", axis=2, tiled=True)
+    full_in = jnp.concatenate(all_gather(w_in, "head"), axis=2)
     full_fx = lax.all_gather(w_fx, "head", axis=2, tiled=True)
     full_out = lax.all_gather(w_out, "head", axis=1, tiled=True)
     heads = full_in.shape[2] // DH

time: 159 us -> 164 us (1.031)
  matrix products: 27.6 us -> 32.3 us
  other arithmetic: 12.6 us -> 8.35 us
  local copies, waits for them, and re-layouts: 8.79 us -> 12.7 us
    dot_general x2, matrix products: 1.2 us -> 4.24 us  [body(): jnp.einsum('rs,rl->sl', half_weights, feats, preferred_element_type=jnp.f...]
    all_gather x1, blocking collectives: 8.21 us -> 11.1 us  [body(): full_fx = lax.all_gather(w_fx, 'head', axis=2, tiled=True)]
    reduce_sum x2, other arithmetic: 3.22 us -> 0.44 us  [body(): total = jnp.sum(weights, axis=0)]
    all_gather x1, blocking collectives: 9.72 us -> 7.44 us  [body(): full_in = jnp.concatenate(all_gather(w_in, 'head'), axis=2)]
where the time goes in v1:
time: 164 us; the launch traced here: 163 us
  blocking collectives  108 us (66%)
  matrix products  32.3 us (20%)
  local copies, waits for them, and re-layouts  12.7 us (8%)
  other arithmetic  8.35 us (5%)
    psum x2, blocking collectives, body(): numerator, total = lax.psum((numerator, total), ('pts', 'head'))  81.5 us
    all_gather x1, blocking collectives, body(): full_fx = lax.all_gather(w_fx, 'head', axis=2, tiled=True)  11.1 us
    dot_general x2, matrix products, body(): jnp.dot(upper, w_down[layer_index], preferred_element_type=jnp.float32)  8.51 us
    all_gather x1, blocking collectives, body(): full_out = lax.all_gather(w_out, 'head', axis=1, tiled=True)  8.02 us
    all_gather x1, blocking collectives, body(): full_in = jnp.concatenate(all_gather(w_in, 'head'), axis=2)  7.44 us
    dot_general x2, matrix products, body(): projected = jnp.dot(half_weights, wide, preferred_element_type=jnp.float32)  6.22 us
    sub x2, matrix products, body(): weights = jax.nn.softmax(logits, axis=-1) * live[:, None, None]  5.29 us
    dot_general x2, matrix products, body(): jnp.einsum('rs,rl->sl', half_weights, feats, preferred_element_type=jnp.f...  4.24 us

profile of v1, /device:TPU:0, one launch (start us, length us, event | category | flops | bytes accessed | tf_op | source)
XLA Modules:
  0.0 162.5 jit_solution(15274077115372126511)
XLA Ops:
  0.8 1.3 slice_bitcast_fusion.17
  2.2 1.3 slice_bitcast_fusion.16
  3.5 1.3 slice_bitcast_fusion.18
  4.7 1.3 slice_bitcast_fusion.14
  6.1 0.7 slice_bitcast_fusion.12
  7.0 11.1 %all_gather.14 = bf16[2,128,128]{1,2,0:T(8,128)(2,1)} all-gather(bf16[2,128,32]{1,2,0:T(8,128)(2,1)} %param.22), channel_id=1, replica_groups=mesh['pts'=8,'head'=4] {'head'}, dimensions={2}, use_global_device_ids=true | all-gather | bytes 81920 | tf_op jit(solution)/shard_map/all_gather | solution.py:58
  18.1 7.4 %all-gather = bf16[8,128,32]{1,2,0:T(8,128)(2,1)S(1)} all-gather(bf16[2,128,32]{1,2,0:T(8,128)(2,1)} %param.21), channel_id=2, replica_groups=mesh['pts'=8,'head'=4] {'head'}, dimensions={0}, use_global_device_ids=true | all-gather | bytes 81920 | tf_op jit(solution)/shard_map/all_gather | solution.py:57
  26.2 8.0 %all_gather.15 = bf16[2,128,128]{2,1,0:T(8,128)(2,1)S(1)} all-gather(bf16[2,32,128]{2,1,0:T(8,128)(2,1)} %param.28), channel_id=1, replica_groups=mesh['pts'=8,'head'=4] {'head'}, dimensions={1}, use_global_device_ids=true | all-gather | bytes 81920 | tf_op jit(solution)/shard_map/all_gather | solution.py:59
  35.0 0.7 mul.210
  35.7 0.7 mul.187
  37.6 1.2 convolution_convert_fusion.1
  38.8 1.9 %fusion.124 = (f32[2304,4]{0,1:T(4,128)S(1)}, f32[2304,4,32]{0,2,1:T(8,128)}) fusion(bf16[4,32,128]{2,1,0:T(8,128)(2,1)S(1)} %bitcast.194, bf16[128,128]{0,1:T(8,128)(2,1)S(1)} %bitcast.198, f32[4]{0:T(128)S(1)} %copy-done.15, bf16[2304,128]{0,1:T(8,128)(2,1)S(1)} %copy.31, f32[128]{0:T(128)S(1)} %copy-done.17, f32[128]{0:T(128)S(1)} %copy-done.18, ...), kind=kOutput, calls=%fused_computation.173 | convolution fusion | flops 153944096 | bytes 1891344 | tf_op jit(solution)/shard_map/sub | solution.py:76
  40.7 2.1 %fusion.39 = f32[4,32,4,32]{3,1,2,0:T(8,128)S(1)} fusion(bf16[4,32,2304,1]{2,1,0,3:T(8,128)(2,1)} %bitcast.199, f32[2304]{0:T(1024)S(1)} %fusion.81, f32[2304,4,32]{0,2,1:T(8,128)} %get-tuple-element.38, f32[2304,4]{0,1:T(4,128)S(1)} %get-tuple-element.37), kind=kOutput, calls=%fused_computation.67 | convolution fusion | flops 76382208 | bytes 1881088 | tf_op jit(solution)/shard_map/rs,rl->sl/dot_general | solution.py:79
  43.1 40.2 %all-reduce.1 = (f32[4,32,32]{2,1,0:T(8,128)S(1)}, f32[4,32]{1,0:T(4,128)S(1)}) all-reduce(f32[4,32,32]{2,1,0:T(8,128)S(1)} %pad_maximum_fusion, f32[4,32]{1,0:T(4,128)S(1)} %fusion.57), channel_id=1, replica_groups=mesh['pts'=8,'head'=4] {'pts','head'}, use_global_device_ids=true, to_apply=%region_4.5 | all-reduce | flops 4224 | bytes 33792 | tf_op jit(solution)/shard_map/psum | solution.py:82
  84.7 2.8 %fusion.128 = (f32[2304]{0:T(1024)S(1)}, f32[2304,128]{0,1:T(8,128)}) fusion(f32[128]{0:T(128)S(1)} %copy-done.14, bf16[4,32,32]{2,1,0:T(8,128)(2,1)S(1)} %convolution_convert_fusion.7, bf16[4,32,128]{2,1,0:T(8,128)(2,1)S(1)} %bitcast.197, f32[2304]{0:T(1024)S(1)} %fusion.81, f32[2304,4,32]{0,2,1:T(8,128)} %get-tuple-element.38, ...), kind=kOutput, calls=%fused_computation.175 | convolution fusion | flops 78624512 | bytes 3045888 | tf_op jit(solution)/shard_map/dot_general | solution.py:100
  87.5 1.4 multiply_reduce_fusion.2
  89.5 4.5 %fusion.129 = (f32[2304]{0:T(1024)}, f32[2304,128]{0,1:T(8,128)S(1)}) fusion(f32[2304,128]{0,1:T(8,128)} %get-tuple-element.42, bf16[2,512,128]{2,1,0:T(8,128)(2,1)} %param.33, f32[128]{0:T(128)} %get-tuple-element.26, f32[128]{0:T(128)} %get-tuple-element.53, f32[2304]{0:T(1024)} %add_rsqrt_fusion.2, f32[2304]{0:T(1024)} %copy-done.7, ...), kind=kOutput, calls=%fused_computation.176 | convolution fusion | flops 617248512 | bytes 3835904 | tf_op jit(solution)/shard_map/dot_general | solution.py:109
  94.1 0.7 broadcast_multiply_fusion.3
  95.4 0.8 copy-done.1
  96.2 1.1 convolution_convert_fusion
  97.3 3.4 %fusion.132 = (f32[2304,4]{0,1:T(4,128)}, f32[2304,4,32]{0,2,1:T(8,128)}) fusion(bf16[4,32,128]{2,1,0:T(8,128)(2,1)} %bitcast.193, bf16[2304,128]{0,1:T(8,128)(2,1)} %copy-done.1, bf16[128,128]{0,1:T(8,128)(2,1)} %bitcast.196, f32[4]{0:T(128)S(1)} %copy-done.13), kind=kOutput, calls=%fused_computation.177 | convolution fusion | flops 152174624 | bytes 1871888 | tf_op jit(solution)/shard_map/sub | solution.py:76
  100.8 2.1 %fusion.37 = f32[4,32,4,32]{3,1,2,0:T(8,128)S(1)} fusion(bf16[4,32,2304,1]{2,1,0,3:T(8,128)(2,1)} %bitcast.191, f32[2304]{0:T(1024)S(1)} %fusion.81, f32[2304,4,32]{0,2,1:T(8,128)} %get-tuple-element.46, f32[2304,4]{0,1:T(4,128)} %get-tuple-element.45), kind=kOutput, calls=%fused_computation.65 | convolution fusion | flops 76382208 | bytes 1881088 | tf_op jit(solution)/shard_map/rs,rl->sl/dot_general | solution.py:79
  103.8 41.3 %all-reduce = (f32[4,32,32]{2,1,0:T(8,128)}, f32[4,32]{1,0:T(4,128)}) all-reduce(f32[4,32,32]{2,1,0:T(8,128)} %pad_maximum_fusion.1, f32[4,32]{1,0:T(4,128)S(1)} %fusion.59), channel_id=1, replica_groups=mesh['pts'=8,'head'=4] {'pts','head'}, use_global_device_ids=true, to_apply=%region_15.16 | all-reduce | flops 4224 | bytes 33792 | tf_op jit(solution)/shard_map/psum | solution.py:82
  145.7 1.1 fusion.84
  146.8 1.1 fusion.82
  147.9 1.1 fusion.86
  149.3 0.9 convolution_convert_fusion.5
  150.2 3.4 %fusion.134 = (f32[2304]{0:T(1024)}, f32[2304,128]{0,1:T(8,128)}) fusion(f32[128]{0:T(128)} %get-tuple-element.27, f32[2304,128]{0,1:T(8,128)S(1)} %get-tuple-element.44, bf16[4,32,32]{2,1,0:T(8,128)(2,1)} %convolution_convert_fusion.5, bf16[4,32,128]{2,1,0:T(8,128)(2,1)} %bitcast.195, f32[2304]{0:T(1024)S(1)} %fusion.81, ...), kind=kOutput, calls=%fused_computation.179 | convolution fusion | flops 78329600 | bytes 3635712 | tf_op jit(solution)/shard_map/dot_general | solution.py:100
  153.6 0.8 broadcast_multiply_fusion.2
  154.4 1.4 multiply_reduce_fusion
  156.5 4.0 %fusion.27 = bf16[2304,128]{0,1:T(8,128)(2,1)} fusion(f32[2304,128]{0,1:T(8,128)S(1)} %copy-done.4, f32[128]{0:T(128)S(1)} %copy-done.16, f32[128]{0:T(128)} %get-tuple-element.54, f32[2304]{0:T(1024)} %add_rsqrt_fusion, f32[2304]{0:T(1024)S(1)} %broadcast_multiply_fusion.2, bf16[2,512,128]{2,1,0:T(8,128)(2,1)} %param.33, bf16[2,128,512]{2,1,0:T(8,128)(2,1)} %param.32), kind=kOutput, calls=%fused_computation.35 | convolution fusion | flops 616660992 | bytes 3236864 | tf_op jit(solution)/shard_map/dot_general | solution.py:109
  160.4 2.1 %copy.27 = bf16[2304,128]{1,0:T(8,128)(2,1)} copy(bf16[2304,128]{0,1:T(8,128)(2,1)} %fusion.27) | data formatting | bytes 1179648 | tf_op jit(solution)/shard_map/convert_element_type | solution.py:110
  (78 shorter events, 7.8 us)
Async XLA Ops:
  0.0 36.4 %copy-start = (bf16[9216,128]{1,0:T(8,128)(2,1)S(1)}, bf16[9216,128]{1,0:T(8,128)(2,1)}, u32[]{:S(2)}) copy-start(bf16[9216,128]{1,0:T(8,128)(2,1)} %param.17) | copy-start | bytes 7077892
  36.7 0.8 copy-start.5
  36.7 0.8 copy-start.17
  36.8 0.8 copy-start.18
  36.9 2.0 %copy-start.9 = (bf16[128,128]{0,1:T(8,128)(2,1)S(1)}, bf16[128,128]{0,1:T(8,128)(2,1)}, u32[]{:S(2)}) copy-start(bf16[128,128]{0,1:T(8,128)(2,1)} %mul.187) | copy-start | bytes 98308
  36.9 1.9 %copy-start.11 = (bf16[1,128,4,32]{1,3,0,2:T(8,128)(2,1)S(1)}, bf16[1,128,4,32]{1,3,0,2:T(8,128)(2,1)}, u32[]{:S(2)}) copy-start(bf16[1,128,4,32]{1,3,0,2:T(8,128)(2,1)} %get-tuple-element.20) | copy-start | bytes 98308
  36.9 1.9 %copy-start.15 = (f32[4]{0:T(128)S(1)}, f32[4]{0:T(128)}, u32[]{:S(2)}) copy-start(f32[4]{0:T(128)} %get-tuple-element.30) | copy-start | bytes 52
  40.7 2.2 %copy-start.2 = (f32[2304,4,32]{0,2,1:T(8,128)S(1)}, f32[2304,4,32]{0,2,1:T(8,128)}, u32[]{:S(2)}) copy-start(f32[2304,4,32]{0,2,1:T(8,128)} %get-tuple-element.38) | copy-start | bytes 3538948
  42.8 40.5 %copy-start.19 = (bf16[2,32,32]{2,1,0:T(8,128)(2,1)S(1)}, bf16[2,32,32]{2,1,0:T(8,128)(2,1)}, u32[]{:S(2)}) copy-start(bf16[2,32,32]{2,1,0:T(8,128)(2,1)} %param.26) | copy-start | bytes 12292
  42.8 40.8 %copy-start.20 = (bf16[2,32,32]{2,1,0:T(8,128)(2,1)S(1)}, bf16[2,32,32]{2,1,0:T(8,128)(2,1)}, u32[]{:S(2)}) copy-start(bf16[2,32,32]{2,1,0:T(8,128)(2,1)} %param.27) | copy-start | bytes 12292
  42.8 41.0 %copy-start.21 = (bf16[2,32,32]{2,1,0:T(8,128)(2,1)S(1)}, bf16[2,32,32]{2,1,0:T(8,128)(2,1)}, u32[]{:S(2)}) copy-start(bf16[2,32,32]{2,1,0:T(8,128)(2,1)} %param.25) | copy-start | bytes 12292
  42.9 41.8 %copy-start.10 = (bf16[1,128,128]{2,1,0:T(8,128)(2,1)S(1)}, bf16[1,128,128]{2,1,0:T(8,128)(2,1)}, u32[]{:S(2)}) copy-start(bf16[1,128,128]{2,1,0:T(8,128)(2,1)} %get-tuple-element.18) | copy-start | bytes 98308
  42.9 41.8 %copy-start.14 = (f32[128]{0:T(128)S(1)}, f32[128]{0:T(128)}, u32[]{:S(2)}) copy-start(f32[128]{0:T(128)} %get-tuple-element.28) | copy-start | bytes 1540
  87.5 1.4 copy-start.7
  94.1 0.9 copy-start.12
  94.9 1.3 copy-start.6
  95.3 0.8 copy-start.1
  96.2 1.1 copy-start.13
  100.7 2.8 %copy-start.3 = (f32[2304,4,32]{0,2,1:T(8,128)S(1)}, f32[2304,4,32]{0,2,1:T(8,128)}, u32[]{:S(2)}) copy-start(f32[2304,4,32]{0,2,1:T(8,128)} %get-tuple-element.46) | copy-start | bytes 3538948
  100.7 2.8 %copy-start.8 = (f32[2304,4]{0,1:T(4,128)S(1)}, f32[2304,4]{0,1:T(4,128)}, u32[]{:S(2)}) copy-start(f32[2304,4]{0,1:T(4,128)} %get-tuple-element.45) | copy-start | bytes 110596
  153.6 2.8 %copy-start.4 = (f32[2304,128]{0,1:T(8,128)S(1)}, f32[2304,128]{0,1:T(8,128)}, u32[]{:S(2)}) copy-start(f32[2304,128]{0,1:T(8,128)} %get-tuple-element.50) | copy-start | bytes 3538948
  153.6 2.8 %copy-start.16 = (f32[128]{0:T(128)S(1)}, f32[128]{0:T(128)}, u32[]{:S(2)}) copy-start(f32[128]{0:T(128)} %get-tuple-element.25) | copy-start | bytes 1540
